TPU v7x, 32 devices: a whole 2x2x4 slice. The times are simulated.
32 devices in a mesh: node: 16 (over z, y, x), hand: 2 (over core).
Axes of the slice: x: 2, y: 2, z: 4, core: 2. Of those that a mesh axis runs over, the one named last changes fastest.
Arguments:
- ranges: bfloat16 [512, 128, 1326], P('node', None, 'hand'), may hold values from 0.00019931793 to 0.0039978027
- strengths: int32 [512, 1326], P('node'), may hold values from 0 to 399
- live_hands: int32 [512, 1326], P('node'), may hold values 0 or 1
- pot_sizes: float32 [512, 128], P('node'), may hold values from 1 to 16
- action_counts: int32 [512], P('node'), may hold values from 1 to 8
- parents: int32 [512], P('node'), may hold values from 0 to 63
- turn_counts: int32 [16], replicated, may hold values from 1 to 4
- root_reach: float32 [16, 2, 1326], P(None, None, 'hand'), may hold values from 0.01 to 1
Outputs:
- turn_values: float32 [16, 2, 1326], P('node', None, 'hand')
- exploitability: float32 [], replicated
All inputs are finite; a program needn't handle non-finite values. No bound on the sum of `live_hands` on one device may be relied on, other than what follows from the above.
Results may differ from a plain program's by a relative error of at most 0.0003.
Values may be sent and summed in bfloat16 or wider, within the bound.
A program may use at most 128 MiB of HBM per device.

v0:
```python
import jax
import jax.numpy as jnp
import numpy as np
from jax import lax
from jax.sharding import PartitionSpec as P

ACT = 8
GROUPS = 8
TACT = 4


def card_pairs(wanted):
    first_list = []
    second_list = []
    for lower_card in range(52):
        for upper_card in range(lower_card + 1, 52):
            first_list.append(lower_card)
            second_list.append(upper_card)
    return (
        jnp.asarray(np.array(first_list[:wanted], dtype=np.int32)),
        jnp.asarray(np.array(second_list[:wanted], dtype=np.int32)),
    )


def pair_compat(row_first, row_second, col_first, col_second):
    shared = (row_first[:, None] == col_first[None, :]) | (
        row_first[:, None] == col_second[None, :]
    )
    shared = (
        shared
        | (row_second[:, None] == col_first[None, :])
        | (row_second[:, None] == col_second[None, :])
    )
    return jnp.where(shared, 0.0, 1.0).astype(jnp.float32)


def showdown_block(compat, packed):
    left_strength, left_live, right_strength, right_live, reach_block = packed
    signs = jnp.sign((left_strength[:, :, None] - right_strength[:, None, :]).astype(jnp.float32))
    matrix = (signs * compat[None] * left_live[:, :, None] * right_live[:, None, :]).astype(
        jnp.bfloat16
    )
    return jnp.einsum("nij,nlj->nli", matrix, reach_block, preferred_element_type=jnp.float32)


def river_from(raw_values, pots, legal):
    count = raw_values.shape[0]
    width = raw_values.shape[2]
    values = (raw_values * pots[:, :, None]).reshape(count, 2, GROUPS, ACT, width)
    usable = jnp.arange(ACT)[None, :] < legal[:, None]
    return jnp.where(usable[:, None, None, :, None], values, -1e30).max(axis=3).sum(axis=2)


def turn_best(sums, legal):
    hand_half = sums.shape[1] // 2
    shaped = sums.reshape(-1, TACT, 2, hand_half)
    usable = jnp.arange(TACT)[None, :] < legal[:, None]
    return jnp.where(usable[:, :, None, None], shaped, -1e30).max(axis=1)


def local(
    ranges, strengths, live_hands, pot_sizes, action_counts, parents, turn_counts, root_reach
):
    node_count, line_cols, hand_half = ranges.shape
    hands_all = strengths.shape[1]
    hand_start = lax.axis_index("hand") * hand_half
    first_card, second_card = card_pairs(hands_all)
    live_all = live_hands.astype(jnp.float32)
    blocks = node_count // 4

    def grouped(array):
        return array.reshape((blocks, 4) + array.shape[1:])

    row_first = lax.dynamic_slice_in_dim(first_card, hand_start, hand_half, 0)
    row_second = lax.dynamic_slice_in_dim(second_card, hand_start, hand_half, 0)
    row_strength = lax.dynamic_slice_in_dim(strengths, hand_start, hand_half, 1)
    row_live = lax.dynamic_slice_in_dim(live_all, hand_start, hand_half, 1)
    compat = pair_compat(row_first, row_second, first_card, second_card)

    def one_block(packed):
        return showdown_block(compat, packed)

    added = lax.map(
        one_block,
        (
            grouped(row_strength),
            grouped(row_live),
            grouped(strengths),
            grouped(live_all),
            grouped(lax.all_gather(ranges, "hand", axis=2, tiled=True)),
        ),
    )
    raw_values = added.reshape(jnp.zeros((node_count, line_cols, hand_half), jnp.float32).shape)
    river_best = river_from(raw_values, pot_sizes, action_counts)
    flat_best = river_best.reshape(node_count, 2 * hand_half)
    turns_all = turn_counts.shape[0]
    turns_mine = turns_all // lax.axis_size("node")
    turn_start = lax.axis_index("node") * turns_mine
    parents_all = turns_all * TACT
    onehot = (parents[None, :] == jnp.arange(parents_all, dtype=jnp.int32)[:, None]).astype(
        jnp.float32
    )
    local_sums = jnp.dot(onehot, flat_best, precision=lax.Precision.HIGHEST)
    totals = lax.psum(local_sums, "node")
    values_all = turn_best(totals, turn_counts)
    exploitability = lax.psum(jnp.sum(root_reach * values_all), "hand")
    turn_values = lax.dynamic_slice_in_dim(values_all, turn_start, turns_mine, 0)
    return (turn_values, exploitability)


def solution(mesh):
    in_specs = (
        P("node", None, "hand"),
        P("node", None),
        P("node", None),
        P("node", None),
        P("node"),
        P("node"),
        P(),
        P(None, None, "hand"),
    )
    out_specs = (P("node", None, "hand"), P())
    return jax.shard_map(local, mesh=mesh, in_specs=in_specs, out_specs=out_specs, check_vma=False)
```

profile of v0, /device:TPU:0, one launch (start us, length us, event | category | flops | bytes accessed | tf_op | source)
XLA Modules:
  0.0 278.7 jit_solution(3800787151186367840)
XLA Ops:
  14.4 20.9 %all-gather.2.cloned.1.call-done = bf16[32,128,1326]{1,0,2:T(8,128)(2,1)} async-done(((bf16[32,128,663]{1,0,2:T(8,128)(2,1)}), bf16[32,128,1326]{1,0,2:T(8,128)(2,1)}) %all-gather.2.cloned.1.call-update) | async-done | bytes 10862608 | tf_op jit(solution)/shard_map/all_gather | solution.py:90
  35.3 89.9 %while.11 = (s32[]{:T(128)}, f32[8,4,128,663]{2,3,1,0:T(8,128)}, bf16[8,4,128,1326]{2,1,0,3:T(4,128)(2,1)}, s32[8,4,663]{2,1,0:T(4,128)S(1)}, s32[8,4,1326]{2,1,...) while((s32[]{:T(128)}, f32[8,4,128,663]{2,3,1,0:T(8,128)}, ...), condition=%wide.region_1.2_spmd.clone, body=%wide.region_0.1_spmd.clone.sunk | while | flops 931886272 | bytes 12673953 | solution.py:83
  35.3 1.6 constant_dynamic-slice_fusion.5
  37.0 2.2 or_select_fusion.2
  39.2 7.4 %fusion.9 = f32[8,4,128,663]{2,3,1,0:T(8,128)} fusion(f32[8,4,128,663]{2,3,1,0:T(8,128)} %get-tuple-element.197, s32[]{:T(128)} %get-tuple-element.196, f32[4,1326]{1,0:T(4,128)S(1)} %dynamic-slice_bitcast_fusion.8, f32[4,663]{1,0:T(4,128)S(1)} %dynamic-slice_bitcast_fusion.9, f32[663,1326]{1,0:T(8,128)S(1)} %or_select_fusion.2, ...), kind=kOutput, calls=%fused_computation.5.clone.1 | convolution fusion | flops 924853184 | bytes 6298408 | tf_op jit(solution)/shard_map/while/body/eval_jaxpr/nij,nlj->nli/dot_general | solution.py:43
  46.6 1.6 constant_dynamic-slice_fusion.5
  48.3 2.2 or_select_fusion.2
  50.5 7.3 %fusion.9 = f32[8,4,128,663]{2,3,1,0:T(8,128)} fusion(f32[8,4,128,663]{2,3,1,0:T(8,128)} %get-tuple-element.197, s32[]{:T(128)} %get-tuple-element.196, f32[4,1326]{1,0:T(4,128)S(1)} %dynamic-slice_bitcast_fusion.8, f32[4,663]{1,0:T(4,128)S(1)} %dynamic-slice_bitcast_fusion.9, f32[663,1326]{1,0:T(8,128)S(1)} %or_select_fusion.2, ...), kind=kOutput, calls=%fused_computation.5.clone.1 | convolution fusion | flops 924853184 | bytes 6298408 | tf_op jit(solution)/shard_map/while/body/eval_jaxpr/nij,nlj->nli/dot_general | solution.py:43
  57.8 1.6 constant_dynamic-slice_fusion.5
  59.5 2.2 or_select_fusion.2
  61.7 7.3 %fusion.9 = f32[8,4,128,663]{2,3,1,0:T(8,128)} fusion(f32[8,4,128,663]{2,3,1,0:T(8,128)} %get-tuple-element.197, s32[]{:T(128)} %get-tuple-element.196, f32[4,1326]{1,0:T(4,128)S(1)} %dynamic-slice_bitcast_fusion.8, f32[4,663]{1,0:T(4,128)S(1)} %dynamic-slice_bitcast_fusion.9, f32[663,1326]{1,0:T(8,128)S(1)} %or_select_fusion.2, ...), kind=kOutput, calls=%fused_computation.5.clone.1 | convolution fusion | flops 924853184 | bytes 6298408 | tf_op jit(solution)/shard_map/while/body/eval_jaxpr/nij,nlj->nli/dot_general | solution.py:43
  69.0 1.6 constant_dynamic-slice_fusion.5
  70.7 2.2 or_select_fusion.2
  73.0 7.3 %fusion.9 = f32[8,4,128,663]{2,3,1,0:T(8,128)} fusion(f32[8,4,128,663]{2,3,1,0:T(8,128)} %get-tuple-element.197, s32[]{:T(128)} %get-tuple-element.196, f32[4,1326]{1,0:T(4,128)S(1)} %dynamic-slice_bitcast_fusion.8, f32[4,663]{1,0:T(4,128)S(1)} %dynamic-slice_bitcast_fusion.9, f32[663,1326]{1,0:T(8,128)S(1)} %or_select_fusion.2, ...), kind=kOutput, calls=%fused_computation.5.clone.1 | convolution fusion | flops 924853184 | bytes 6298408 | tf_op jit(solution)/shard_map/while/body/eval_jaxpr/nij,nlj->nli/dot_general | solution.py:43
  80.2 1.6 constant_dynamic-slice_fusion.5
  81.9 2.2 or_select_fusion.2
  84.2 7.3 %fusion.9 = f32[8,4,128,663]{2,3,1,0:T(8,128)} fusion(f32[8,4,128,663]{2,3,1,0:T(8,128)} %get-tuple-element.197, s32[]{:T(128)} %get-tuple-element.196, f32[4,1326]{1,0:T(4,128)S(1)} %dynamic-slice_bitcast_fusion.8, f32[4,663]{1,0:T(4,128)S(1)} %dynamic-slice_bitcast_fusion.9, f32[663,1326]{1,0:T(8,128)S(1)} %or_select_fusion.2, ...), kind=kOutput, calls=%fused_computation.5.clone.1 | convolution fusion | flops 924853184 | bytes 6298408 | tf_op jit(solution)/shard_map/while/body/eval_jaxpr/nij,nlj->nli/dot_general | solution.py:43
  91.5 1.6 constant_dynamic-slice_fusion.5
  93.2 2.2 or_select_fusion.2
  95.4 7.3 %fusion.9 = f32[8,4,128,663]{2,3,1,0:T(8,128)} fusion(f32[8,4,128,663]{2,3,1,0:T(8,128)} %get-tuple-element.197, s32[]{:T(128)} %get-tuple-element.196, f32[4,1326]{1,0:T(4,128)S(1)} %dynamic-slice_bitcast_fusion.8, f32[4,663]{1,0:T(4,128)S(1)} %dynamic-slice_bitcast_fusion.9, f32[663,1326]{1,0:T(8,128)S(1)} %or_select_fusion.2, ...), kind=kOutput, calls=%fused_computation.5.clone.1 | convolution fusion | flops 924853184 | bytes 6298408 | tf_op jit(solution)/shard_map/while/body/eval_jaxpr/nij,nlj->nli/dot_general | solution.py:43
  102.7 1.6 constant_dynamic-slice_fusion.5
  104.4 2.2 or_select_fusion.2
  106.7 7.3 %fusion.9 = f32[8,4,128,663]{2,3,1,0:T(8,128)} fusion(f32[8,4,128,663]{2,3,1,0:T(8,128)} %get-tuple-element.197, s32[]{:T(128)} %get-tuple-element.196, f32[4,1326]{1,0:T(4,128)S(1)} %dynamic-slice_bitcast_fusion.8, f32[4,663]{1,0:T(4,128)S(1)} %dynamic-slice_bitcast_fusion.9, f32[663,1326]{1,0:T(8,128)S(1)} %or_select_fusion.2, ...), kind=kOutput, calls=%fused_computation.5.clone.1 | convolution fusion | flops 924853184 | bytes 6298408 | tf_op jit(solution)/shard_map/while/body/eval_jaxpr/nij,nlj->nli/dot_general | solution.py:43
  113.9 1.6 constant_dynamic-slice_fusion.5
  115.6 2.2 or_select_fusion.2
  117.9 7.3 %fusion.9 = f32[8,4,128,663]{2,3,1,0:T(8,128)} fusion(f32[8,4,128,663]{2,3,1,0:T(8,128)} %get-tuple-element.197, s32[]{:T(128)} %get-tuple-element.196, f32[4,1326]{1,0:T(4,128)S(1)} %dynamic-slice_bitcast_fusion.8, f32[4,663]{1,0:T(4,128)S(1)} %dynamic-slice_bitcast_fusion.9, f32[663,1326]{1,0:T(8,128)S(1)} %or_select_fusion.2, ...), kind=kOutput, calls=%fused_computation.5.clone.1 | convolution fusion | flops 924853184 | bytes 6298408 | tf_op jit(solution)/shard_map/while/body/eval_jaxpr/nij,nlj->nli/dot_general | solution.py:43
  125.2 12.0 %copy.22 = f32[8,4,128,663]{3,2,1,0:T(8,128)} copy(f32[8,4,128,663]{2,3,1,0:T(8,128)} %get-tuple-element.44) | data formatting | bytes 21725184 | tf_op jit(solution)/shard_map/while | solution.py:83
  137.1 16.8 %select_reduce_fusion = f32[32,2,8,663]{3,2,1,0:T(8,128)S(1)} fusion(f32[32,2,8,8,663]{4,3,2,1,0:T(8,128)} %bitcast.31, f32[32,2,8,8]{3,2,1,0:T(8,128)S(1)} %copy.24, pred[32,8]{1,0:T(8,128)(4,1)S(1)} %iota_compare_fusion.2), kind=kLoop, calls=%fused_computation.12 | loop fusion | flops 7807488 | bytes 12237056 | tf_op jit(solution)/shard_map/reduce_max | solution.py:51
  154.9 1.1 reshape.95
  156.2 109.9 %all-reduce.2.cloned.1.call-done = f32[16,4,2,663]{3,2,1,0:T(2,128)} async-done(((f32[16,4,2,663]{3,2,1,0:T(2,128)}), f32[16,4,2,663]{3,2,1,0:T(2,128)}) %all-reduce.2.cloned.1.call-update) | async-done | bytes 339472 | tf_op jit(solution)/shard_map/psum | solution.py:104
  266.1 1.4 select_reduce_fusion.1
  268.8 3.1 %psum.15 = f32[]{:T(128)} all-reduce(f32[]{:T(128)} %multiply_reduce_fusion), channel_id=1, replica_groups=mesh['node'=16,'hand'=2] {'hand'}, use_global_device_ids=true, to_apply=%region_7.8 | all-reduce | flops 1 | bytes 8 | tf_op jit(solution)/shard_map/psum | solution.py:106
  (61 shorter events, 9.8 us)
Async XLA Ops:
  7.2 28.1 %all-gather.2.cloned.1.call-start = ((), (), s32[]{:S(2)}) async-start(), calls=%async_computation | async-start | bytes 16293888 | tf_op jit(solution)/shard_map/all_gather | solution.py:90
  7.9 258.2 %all-reduce.2.cloned.1.call-start = ((), (), s32[]{:S(2)}) async-start(), calls=%async_computation.1 | async-start | bytes 786432 | tf_op jit(solution)/shard_map/psum | solution.py:104
  137.1 17.5 %copy-start.1 = (s32[32]{0:T(128)S(1)}, s32[32]{0:T(128)}, u32[]{:S(2)}) copy-start(s32[32]{0:T(128)} %param.17) | copy-start | bytes 388
  137.1 18.9 %copy-start.2 = (s32[16]{0:T(128)S(1)}, s32[16]{0:T(128)}, u32[]{:S(2)}) copy-start(s32[16]{0:T(128)} %param.18) | copy-start | bytes 196
  137.1 130.4 %copy-start = (f32[16,2,663]{2,1,0:T(2,128)S(1)}, f32[16,2,663]{2,1,0:T(2,128)}, u32[]{:S(2)}) copy-start(f32[16,2,663]{2,1,0:T(2,128)} %param.19) | copy-start | bytes 254596
Sparse Core Ops, SparseCore 0:
  9.5 25.7 all-gather.1
  156.2 109.8 all-reduce.1
where the time goes:
time: 280 us; the launch traced here: 279 us
  waiting for transfers between devices  132 us (47%)
  matrix products  58.7 us (21%)
  other arithmetic  39.1 us (14%)
  local copies, waits for them, and re-layouts  31.7 us (11%)
  between operations  14.2 us (5%)
  blocking collectives  3.08 us (1%)
    psum x1, waiting for transfers between devices, local(): totals = lax.psum(local_sums, 'node')  110 us
    dot_general x8, matrix products, showdown_block(): jnp.einsum('nij,nlj->nli', matrix, reach_block, preferred_element_type=jn...  58.4 us
    all_gather x1, waiting for transfers between devices, local(): lax.all_gather(ranges, 'hand', axis=2, tiled=True)  20.9 us
    select_n x8, other arithmetic, pair_compat(): return jnp.where(shared, 0.0, 1.0).astype(jnp.float32)  17.9 us
    reduce_max x1, other arithmetic, river_from(): jnp.where(usable[:, None, None, :, None], values, -1e+30).max(axis=3)  16.8 us
    dynamic_slice x8, local copies, waits for them, and re-layouts, local(): lax.map(one_block, (grouped(row_strength), grouped(row_live), grouped(str...  12.8 us
    while x1, local copies, waits for them, and re-layouts, local(): lax.map(one_block, (grouped(row_strength), grouped(row_live), grouped(str...  12 us
  transfers between devices with their start and end apart: 2, of which 2 were waited for; matrix products, arithmetic and copies ran while one was open for 2% of the time, Pallas kernels for 0%

commit v1 on v0

v1 whole, which is shorter than its diff:
```python
import functools

import jax
import jax.numpy as jnp
import numpy as np
from jax import lax
from jax.experimental import pallas as pl
from jax.experimental.pallas import tpu as pltpu
from jax.sharding import PartitionSpec as P

ACT = 8
GROUPS = 8
TACT = 4
LANE = 128
MESH = pl.DeviceIdType.MESH
GROUP = 4
MID = 200.0
LOW = -1e30


def card_rows(hands, half, padded):
    pairs = [(a, b) for a in range(52) for b in range(a + 1, 52)][:hands]
    flat = np.array(pairs, np.float32).T
    rows = np.zeros((2, 8, padded), np.float32)
    for part in range(2):
        rows[part, :2, :half] = flat[:, part * half : (part + 1) * half]
    return jnp.asarray(rows)


def kernel(
    sizes,
    ranges,
    strengths,
    live,
    pots,
    legal,
    parents,
    turn_legal,
    reach,
    cards,
    best_out,
    total_out,
    held,
    row_s,
    row_live,
    col_s,
    col_pot,
    compat,
    signs,
    lines,
    river,
    part,
    got,
    shares,
    local_sem,
    send_sem,
    recv_sem,
    out_sem,
    in_sem,
    tell_sem,
    told_sem,
):
    n_node, nodes, half, padded, turns_mine, rows_all = sizes
    f32, bf16 = jnp.float32, jnp.bfloat16
    node = lax.axis_index("node")
    hand = lax.axis_index("hand")
    me = node * 2 + hand
    n_dev = 2 * n_node
    line_cols = lines.shape[1]
    steps = nodes // GROUP

    barrier = pltpu.get_barrier_semaphore()

    def greet(offset, carry):
        other = lax.rem(me + offset, n_dev)
        pl.semaphore_signal(
            barrier,
            inc=1,
            device_id=(other // 2, lax.rem(other, 2)),
            device_id_type=MESH,
        )
        return carry

    lax.fori_loop(1, n_dev, greet, 0)

    def local_copy(step):
        span = pl.ds(step * GROUP, GROUP)
        return pltpu.make_async_copy(
            ranges.at[span], held.at[hand, span], local_sem.at[step]
        )

    def peer_copy(step):
        span = pl.ds(step * GROUP, GROUP)
        return pltpu.make_async_remote_copy(
            src_ref=ranges.at[span],
            dst_ref=held.at[hand, span],
            send_sem=send_sem.at[step],
            recv_sem=recv_sem.at[step],
            device_id=(node, 1 - hand),
            device_id_type=MESH,
        )

    for step in range(steps):
        local_copy(step).start()

    row_s[...] = jnp.zeros_like(row_s)
    strength = strengths[...].astype(f32) - MID
    alive = live[...].astype(f32)
    for side in range(2):
        cut = slice(side * half, (side + 1) * half)
        row_s[side, :nodes, :half] = strength[:, cut]
        row_s[side, nodes : nodes + 8, :] = cards[side]
        row_live[side, :, :half] = alive[:, cut]
    lines[...] = jnp.zeros_like(lines)

    pl.semaphore_wait(barrier, n_dev - 1)
    for step in range(steps):
        peer_copy(step).start()

    for side in range(2):
        for tile in range(padded // LANE):
            block = row_s[side, :, tile * LANE : (tile + 1) * LANE]
            at = side * padded + tile * LANE
            col_s[at : at + LANE, :] = block.T
    pot_block = jnp.concatenate(
        [pots[...], jnp.zeros((LANE - nodes, line_cols), f32)], axis=0
    )
    col_pot[...] = pot_block.T

    hero_first = row_s[hand, nodes : nodes + 1, :]
    hero_second = row_s[hand, nodes + 1 : nodes + 2, :]

    def compat_rows(tile, carry):
        at = pl.ds(pl.multiple_of(tile * LANE, LANE), LANE)
        first = jnp.broadcast_to(col_s[at, nodes : nodes + 1], (LANE, LANE))
        second = jnp.broadcast_to(col_s[at, nodes + 1 : nodes + 2], (LANE, LANE))
        for column in range(padded // LANE):
            cut = slice(column * LANE, (column + 1) * LANE)
            a = hero_first[:, cut]
            b = hero_second[:, cut]
            shared = (first == a) | (first == b) | (second == a) | (second == b)
            compat[at, cut] = jnp.where(shared, 0.0, 1.0).astype(bf16)
        return carry

    lax.fori_loop(0, 2 * padded // LANE, compat_rows, 0)

    def spread(row):
        tall = jnp.broadcast_to(row, (16, LANE)).astype(bf16)
        return jnp.broadcast_to(tall[None], (LANE // 16, 16, LANE)).reshape(LANE, LANE)

    action = lax.broadcasted_iota(jnp.int32, (1, ACT, padded), 1)

    def one_group(step, carry):
        local_copy(step).wait()
        peer_copy(step).wait_recv()
        for first_of in range(0, GROUP, 2):
            pair = (first_of, first_of + 1)
            for u in pair:
                n = step * GROUP + u
                for side in range(2):
                    scaled = held[side, n] * row_live[side, pl.ds(n, 1), :half].astype(bf16)
                    lines[u, :, side * padded : side * padded + half] = scaled
            hero = [row_s[hand, pl.ds(step * GROUP + u, 1), :] for u in pair]
            for tile in range(2 * padded // LANE):
                at = slice(tile * LANE, (tile + 1) * LANE)
                columns = [
                    jnp.broadcast_to(col_s[at, u : u + 1], (LANE, LANE)).astype(bf16)
                    for u in pair
                ]
                for column in range(padded // LANE):
                    cut = slice(column * LANE, (column + 1) * LANE)
                    upper = compat[at, cut]
                    lower = -upper
                    for u, hero_s, column_s in zip(pair, hero, columns):
                        gap = spread(hero_s[:, cut]) - column_s
                        signs[u, at, cut] = jnp.maximum(jnp.minimum(gap, upper), lower)
            for u in pair:
                n = step * GROUP + u
                values = jnp.dot(lines[u], signs[u], preferred_element_type=f32)
                values = values * col_pot[:, u : u + 1]
                values = values.reshape(2 * GROUPS, ACT, padded)
                values = jnp.where(action < legal[n], values, LOW)
                for shift in (4, 2, 1):
                    values = jnp.maximum(values, pltpu.roll(values, shift, 1))
                for player in range(2):
                    best = values[player * GROUPS]
                    for g in range(1, GROUPS):
                        best = best + values[player * GROUPS + g]
                    best = best[:1] * row_live[hand, pl.ds(n, 1), :]
                    river[player, pl.ds(n, 1), :] = best
        col_s[...] = pltpu.roll(col_s[...], LANE - GROUP, 1)
        col_pot[...] = pltpu.roll(col_pot[...], LANE - GROUP, 1)
        return carry

    row_live[:, :, half:] = jnp.zeros((2, nodes, padded - half), f32)
    lax.fori_loop(0, steps, one_group, 0)

    row_at = lax.broadcasted_iota(jnp.int32, (rows_all, nodes), 0)
    wanted = (row_at // (2 * TACT)) * TACT + lax.rem(row_at, TACT)
    match = parents[...] == wanted
    sums = jnp.zeros((rows_all, padded), f32)
    for player in range(2):
        mine = lax.rem(row_at // TACT, 2) == player
        chosen = jnp.where(match & mine, 1.0, 0.0).astype(bf16)
        rest = river[player]
        for _ in range(3):
            piece = rest.astype(bf16)
            sums = sums + jnp.dot(chosen, piece, preferred_element_type=f32)
            rest = rest - piece.astype(f32)
    block_rows = turns_mine * 2 * TACT
    part[...] = sums.reshape(n_node, block_rows, padded)

    def deal(offset):
        other = lax.rem(node + offset, n_node)
        return pltpu.make_async_remote_copy(
            src_ref=part.at[other],
            dst_ref=got.at[offset - 1],
            send_sem=out_sem.at[offset - 1],
            recv_sem=in_sem.at[offset - 1],
            device_id=(other, hand),
            device_id_type=MESH,
        )

    def deal_start(offset, carry):
        deal(offset).start()
        return carry

    lax.fori_loop(1, n_node, deal_start, 0)

    def add_in(offset, total):
        deal(offset).wait_recv()
        return total + got[offset - 1]

    total = lax.fori_loop(1, n_node, add_in, part[node])

    kind = lax.rem(lax.broadcasted_iota(jnp.int32, (2 * TACT, padded), 0), TACT)
    share = jnp.zeros((1, half), f32)
    for t in range(turns_mine):
        turn = node * turns_mine + t
        mine = total[t * 2 * TACT : (t + 1) * 2 * TACT]
        mine = jnp.where(kind < turn_legal[turn], mine, LOW)
        for player in range(2):
            best = jnp.max(mine[player * TACT : (player + 1) * TACT], axis=0, keepdims=True)
            best = best[:, :half]
            best_out[t, player : player + 1, :] = best
            share = share + reach[turn, player : player + 1, :] * best
    shares[me] = jnp.broadcast_to(jnp.sum(share, axis=1, keepdims=True), (8, LANE))

    def tell(offset, back):
        other = lax.rem(me + offset, n_dev)
        source = lax.rem(me + n_dev - offset, n_dev) if back else me
        return pltpu.make_async_remote_copy(
            src_ref=shares.at[me],
            dst_ref=shares.at[source],
            send_sem=tell_sem.at[offset - 1],
            recv_sem=told_sem.at[offset - 1],
            device_id=(other // 2, lax.rem(other, 2)),
            device_id_type=MESH,
        )

    def tell_start(offset, carry):
        tell(offset, False).start()
        return carry

    def tell_wait(offset, carry):
        tell(offset, True).wait_recv()
        return carry

    lax.fori_loop(1, n_dev, tell_start, 0)
    lax.fori_loop(1, n_dev, tell_wait, 0)
    whole = jnp.zeros((8, LANE), f32)
    for device in range(n_dev):
        whole = whole + shares[device]
    total_out[0, 0] = whole[0, 0]

    for step in range(steps):
        peer_copy(step).wait_send()

    def done(offset, carry):
        deal(offset).wait_send()
        return carry

    def done_tell(offset, carry):
        tell(offset, False).wait_send()
        return carry

    lax.fori_loop(1, n_node, done, 0)
    lax.fori_loop(1, n_dev, done_tell, 0)


def solution(mesh):
    n_node = mesh.shape["node"]

    def local(
        ranges, strengths, live_hands, pot_sizes, action_counts, parents, turn_counts, root_reach
    ):
        nodes, line_cols, half = ranges.shape
        hands = strengths.shape[1]
        padded = -(-half // 256) * 256
        turns_all = turn_counts.shape[0]
        turns_mine = turns_all // n_node
        rows_all = turns_all * 2 * TACT
        steps = nodes // GROUP
        f32, bf16 = jnp.float32, jnp.bfloat16
        vmem = pl.BlockSpec(memory_space=pltpu.VMEM)
        smem = pl.BlockSpec(memory_space=pltpu.SMEM)
        hbm = pl.BlockSpec(memory_space=pl.ANY)
        dma = pltpu.SemaphoreType.DMA
        best, total = pl.pallas_call(
            functools.partial(kernel, (n_node, nodes, half, padded, turns_mine, rows_all)),
            out_shape=(
                jax.ShapeDtypeStruct((turns_mine, 2, half), f32),
                jax.ShapeDtypeStruct((1, 1), f32),
            ),
            in_specs=[hbm, vmem, vmem, vmem, smem, vmem, smem, vmem, vmem],
            out_specs=(vmem, smem),
            scratch_shapes=[
                pltpu.VMEM((2, nodes, line_cols, half), bf16),
                pltpu.VMEM((2, LANE, padded), f32),
                pltpu.VMEM((2, nodes, padded), f32),
                pltpu.VMEM((2 * padded, LANE), f32),
                pltpu.VMEM((line_cols, LANE), f32),
                pltpu.VMEM((2 * padded, padded), bf16),
                pltpu.VMEM((GROUP, 2 * padded, padded), bf16),
                pltpu.VMEM((GROUP, line_cols, 2 * padded), bf16),
                pltpu.VMEM((2, nodes, padded), f32),
                pltpu.VMEM((n_node, turns_mine * 2 * TACT, padded), f32),
                pltpu.VMEM((n_node - 1, turns_mine * 2 * TACT, padded), f32),
                pltpu.VMEM((2 * n_node, 8, LANE), f32),
                dma((steps,)),
                dma((steps,)),
                dma((steps,)),
                dma((n_node - 1,)),
                dma((n_node - 1,)),
                dma((2 * n_node - 1,)),
                dma((2 * n_node - 1,)),
            ],
            compiler_params=pltpu.CompilerParams(
                collective_id=0, has_side_effects=True, vmem_limit_bytes=60 * 1024 * 1024
            ),
        )(
            ranges,
            strengths,
            live_hands,
            pot_sizes,
            action_counts,
            parents.reshape(1, nodes),
            turn_counts,
            root_reach,
            card_rows(hands, half, padded),
        )
        return best, total.reshape(())

    in_specs = (
        P("node", None, "hand"),
        P("node", None),
        P("node", None),
        P("node", None),
        P("node"),
        P("node"),
        P(),
        P(None, None, "hand"),
    )
    out_specs = (P("node", None, "hand"), P())
    return jax.shard_map(local, mesh=mesh, in_specs=in_specs, out_specs=out_specs, check_vma=False)
```

time: 280 us -> 76.6 us (0.27)
  waiting for transfers between devices: 132 us -> 0 us
  Pallas kernels: 0 us -> 63.3 us
  matrix products: 58.7 us -> 0 us
  other arithmetic: 39.1 us -> 0 us
  local copies, waits for them, and re-layouts: 31.7 us -> 10.5 us
  between operations: 14.2 us -> 2.4 us
  blocking collectives: 3.08 us -> 0 us
    psum x1 -> x0, waiting for transfers between devices: 110 us -> none  [local(): totals = lax.psum(local_sums, 'node')]
    pallas_call x0 -> x1, Pallas kernels: none -> 63.3 us  [local(): pl.pallas_call(functools.partial(kernel, (n_node, nodes, half, padded, tu...]
    dot_general x9 -> x0, matrix products: 58.7 us -> none  [the longest x8 58.4 us: showdown_block(): jnp.einsum('nij,nlj->nli', matrix, reach_block, preferred_element_type=jn...]
    all_gather x1 -> x0, waiting for transfers between devices: 20.9 us -> none  [local(): lax.all_gather(ranges, 'hand', axis=2, tiled=True)]
    reduce_max x2 -> x0, other arithmetic: 18.2 us -> none  [the longest x1 16.8 us: river_from(): jnp.where(usable[:, None, None, :, None], values, -1e+30).max(axis=3)]
    select_n x8 -> x0, other arithmetic: 17.9 us -> none  [pair_compat(): return jnp.where(shared, 0.0, 1.0).astype(jnp.float32)]
    dynamic_slice x13 -> x0, local copies, waits for them, and re-layouts: 16 us -> none  [the longest x8 12.8 us: local(): lax.map(one_block, (grouped(row_strength), grouped(row_live), grouped(str...]
    while x1 -> x0, local copies, waits for them, and re-layouts: 12 us -> none  [local(): lax.map(one_block, (grouped(row_strength), grouped(row_live), grouped(str...]
  transfers between devices with their start and end apart: 2 -> 0, of which waited for: 2 -> 0; matrix products, arithmetic and copies ran while one was open for 2% -> 0% of each run, Pallas kernels for 0% -> 0%
where the time goes in v1:
time: 76.6 us; the launch traced here: 76.2 us
  Pallas kernels  63.3 us (83%)
  local copies, waits for them, and re-layouts  10.5 us (14%)
  between operations  2.4 us (3%)
    pallas_call x1, Pallas kernels, local(): pl.pallas_call(functools.partial(kernel, (n_node, nodes, half, padded, tu...  63.3 us
    unnamed x2, local copies, waits for them, and re-layouts  10.5 us

profile of v1, /device:TPU:0, one launch (start us, length us, event | category | flops | bytes accessed | tf_op | source)
XLA Modules:
  0.0 76.2 jit_solution(16661303333456931815)
XLA Ops:
  0.6 9.2 %copy.11.ranges = bf16[32,128,663]{2,1,0:T(8,128)(2,1)} copy(bf16[32,128,663]{1,0,2:T(8,128)(2,1)} %param.9) | data formatting | bytes 10862592 | tf_op args[0]
  9.8 63.3 %shard_map.104 = (f32[1,2,663]{2,1,0:T(2,128)}, f32[1,1]{1,0:T(1,128)}) custom-call(bf16[32,128,663]{2,1,0:T(8,128)(2,1)} %copy.11.ranges, s32[32,1326]{1,0:T(8,128)} %strengths.1, s32[32,1326]{1,0:T(8,128)} %live.1, f32[32,128]{1,0:T(8,128)} %pots.1, s32[32]{0:T(128)} %legal.1, s32[1,32]{1,0:T(1,128)} %bitcast.2, s32[16]{0:T(128)} %turn_legal.1, ...), custom_call_target="tpu_custom_call" | custom-call | tf_op jit(solution)/shard_map/pallas_call | solution.py:309
  73.2 1.3 %copy.14 = f32[1,2,663]{2,1,0:T(2,128)} copy(f32[1,2,663]{2,1,0:T(2,128)} %get-tuple-element.8) | data formatting | bytes 10608
